TPU v7x, 32 devices: a 4x4x1 block of a 4x4x8 slice. The times are simulated.
32 devices in a mesh: problem: 1 (over z), samp: 4 (over y), feat: 8 (over x, core).
Axes of the slice: x: 4, y: 4, z: 1, core: 2. Of those that a mesh axis runs over, the one named last changes fastest.
The devices are a block of a 4x4x8 slice.
Arguments:
- design: bfloat16 [16384, 32768], P(('problem', 'samp'), 'feat')
- targets: float32 [16384, 128], P(('problem', 'samp'))
- coef_init: float32 [32768, 128], P(('problem', 'feat'))
- step_sizes: float32 [32768], P(('problem', 'feat'))
- ridge_weights: float32 [128], P('problem')
Outputs:
- output 1: float32 [32768, 128], P(('problem', 'feat'))
- output 2: float32 [16384, 128], P(('problem', 'samp'))
All inputs are finite; a program needn't handle non-finite values.
Results may differ from a plain program's by a relative error of at most 0.00671238.
Values are sent between devices in bfloat16 or wider.
A program may use at most 768 MiB of HBM per device.

v0:
```python
import jax
import jax.numpy as jnp
from jax import lax
from jax.sharding import PartitionSpec as P

SWEEPS = 4
STEP_WEIGHT = 0.5


def solution(mesh):
    samp_size = mesh.shape["samp"]
    design_spec = P(("problem", "samp"), "feat")
    rows_spec = P(("problem", "samp"), None)
    coef_spec = P(("problem", "feat"), None)
    step_spec = P(("problem", "feat"))
    ridge_spec = P("problem")

    def local_sweeps(design, targets, coef_init, step_sizes, ridge_weights):
        total_rows = design.shape[0] * samp_size
        step_col = step_sizes[:, None]
        ridge_row = ridge_weights[None, :]

        def block_product(weights):
            product = jnp.dot(design, weights.astype(jnp.bfloat16), preferred_element_type=jnp.float32)
            return product.astype(jnp.bfloat16).astype(jnp.float32)

        resid_cur = targets - lax.psum(block_product(coef_init), "feat")
        coef_cur = coef_init
        for sweep_index in range(SWEEPS):
            part_grad = lax.dot_general(design, resid_cur.astype(jnp.bfloat16), (((0,), (0,)), ((), ())), preferred_element_type=jnp.float32)
            gradient = lax.psum(part_grad, "samp") / total_rows
            step_delta = step_col * (gradient - ridge_row * coef_cur)
            coef_cur = coef_cur + STEP_WEIGHT * step_delta
            resid_cur = resid_cur - STEP_WEIGHT * lax.psum(block_product(step_delta), "feat")
        return coef_cur, resid_cur

    return jax.shard_map(local_sweeps, mesh=mesh, in_specs=(design_spec, rows_spec, coef_spec, step_spec, ridge_spec), out_specs=(coef_spec, rows_spec), check_vma=False)
```

profile of v0, /device:TPU:97, one launch (start us, length us, event | category | flops | bytes accessed | tf_op | source)
XLA Modules:
  0.0 705.5 jit_solution(17995172835817303217)
XLA Ops:
  7.2 0.1 all-reduce.10.cloned.1.call-start
  7.2 16.7 %fusion.8 = f32[4096,128]{1,0:T(8,128)} fusion(bf16[4096,4096]{1,0:T(8,128)(2,1)} %param.5, f32[4096,128]{1,0:T(8,128)} %param.7), kind=kOutput, calls=%fused_computation.17 | convolution fusion | flops 4296540160 | bytes 37748736 | tf_op jit(solution)/shard_map/dot_general | solution.py:24
  23.9 0.1 all-reduce.10.cloned.1.call-update
  24.0 0.1 all-reduce.12.cloned.1.call-start
  24.0 62.4 %all-reduce.10.cloned.1.call-done = f32[4096,128]{1,0:T(8,128)} async-done(((f32[4096,128]{1,0:T(8,128)}), f32[4096,128]{1,0:T(8,128)}) %all-reduce.10.cloned.1.call-update) | async-done | bytes 2097168 | tf_op jit(solution)/shard_map/psum | solution.py:27
  86.5 2.4 sub.27
  88.9 19.2 %convolution_bitcast_fusion.3 = f32[4096,128]{1,0:T(8,128)} fusion(bf16[4096,4096]{1,0:T(8,128)(2,1)} %param.5, f32[4096,128]{1,0:T(8,128)S(1)} %sub.27), kind=kOutput, calls=%fused_computation.3 | convolution fusion | flops 4295491584 | bytes 37748736 | tf_op jit(solution)/shard_map/dot_general | solution.py:30
  108.1 0.0 copy-start.3
  108.1 0.0 copy-start.4
  108.1 0.1 all-reduce.12.cloned.1.call-update
  108.1 0.2 all-reduce.14.cloned.1.call-start
  108.4 54.6 %all-reduce.12.cloned.1.call-done = f32[4096,128]{1,0:T(8,128)} async-done(((f32[4096,128]{1,0:T(8,128)}), f32[4096,128]{1,0:T(8,128)}) %all-reduce.12.cloned.1.call-update) | async-done | bytes 2097168 | tf_op jit(solution)/shard_map/psum | solution.py:31
  163.0 0.0 copy-done.3
  163.0 0.0 copy-done.4
  163.0 17.3 %fusion.7 = f32[4096,128]{1,0:T(8,128)} fusion(bf16[4096,4096]{1,0:T(8,128)(2,1)} %param.5, f32[4096,128]{1,0:T(8,128)} %param.7, f32[4096,128]{1,0:T(8,128)} %all-reduce.12.cloned.1.call-done, f32[128]{0:T(128)S(1)} %copy-done.4, f32[4096]{0:T(1024)S(1)} %copy-done.3), kind=kOutput, calls=%fused_computation.15 | convolution fusion | flops 4298637312 | bytes 39862784 | tf_op jit(solution)/shard_map/dot_general | solution.py:24
  180.3 0.1 all-reduce.14.cloned.1.call-update
  180.4 0.1 all-reduce.16.cloned.1.call-start
  180.5 58.5 %all-reduce.14.cloned.1.call-done = f32[4096,128]{1,0:T(8,128)} async-done(((f32[4096,128]{1,0:T(8,128)}), f32[4096,128]{1,0:T(8,128)}) %all-reduce.14.cloned.1.call-update) | async-done | bytes 2097168 | tf_op jit(solution)/shard_map/psum | solution.py:34
  239.0 19.6 %convolution_bitcast_fusion.2 = f32[4096,128]{1,0:T(8,128)} fusion(bf16[4096,4096]{1,0:T(8,128)(2,1)} %param.5, f32[4096,128]{1,0:T(8,128)S(1)} %sub.27, f32[4096,128]{1,0:T(8,128)} %all-reduce.14.cloned.1.call-done), kind=kOutput, calls=%fused_computation.2 | convolution fusion | flops 4296540160 | bytes 39845888 | tf_op jit(solution)/shard_map/dot_general | solution.py:30
  258.5 0.1 all-reduce.16.cloned.1.call-update
  258.6 0.3 all-reduce.18.cloned.1.call-start
  258.9 54.5 %all-reduce.16.cloned.1.call-done = f32[4096,128]{1,0:T(8,128)} async-done(((f32[4096,128]{1,0:T(8,128)}), f32[4096,128]{1,0:T(8,128)}) %all-reduce.16.cloned.1.call-update) | async-done | bytes 2097168 | tf_op jit(solution)/shard_map/psum | solution.py:31
  313.4 18.0 %fusion.5 = f32[4096,128]{1,0:T(8,128)} fusion(bf16[4096,4096]{1,0:T(8,128)(2,1)} %param.5, f32[4096,128]{1,0:T(8,128)} %all-reduce.16.cloned.1.call-done, f32[128]{0:T(128)S(1)} %copy-done.4, f32[4096]{0:T(1024)S(1)} %copy-done.3, f32[4096,128]{1,0:T(8,128)} %param.7, f32[4096,128]{1,0:T(8,128)} %all-reduce.12.cloned.1.call-done), kind=kOutput, calls=%fused_computation.12 | convolution fusion | flops 4301783040 | bytes 41959936 | tf_op jit(solution)/shard_map/dot_general | solution.py:24
  331.4 0.1 all-reduce.18.cloned.1.call-update
  331.5 0.1 all-reduce.20.cloned.1.call-start
  331.6 58.6 %all-reduce.18.cloned.1.call-done = f32[4096,128]{1,0:T(8,128)} async-done(((f32[4096,128]{1,0:T(8,128)}), f32[4096,128]{1,0:T(8,128)}) %all-reduce.18.cloned.1.call-update) | async-done | bytes 2097168 | tf_op jit(solution)/shard_map/psum | solution.py:34
  390.1 2.5 multiply_subtract_fusion.2
  392.6 0.0 copy-start
  392.7 1.3 copy-done
  394.0 19.2 %convolution_bitcast_fusion.1 = f32[4096,128]{1,0:T(8,128)} fusion(bf16[4096,4096]{1,0:T(8,128)(2,1)} %param.5, f32[4096,128]{1,0:T(8,128)S(1)} %multiply_subtract_fusion.2), kind=kOutput, calls=%fused_computation.1 | convolution fusion | flops 4295491584 | bytes 37748736 | tf_op jit(solution)/shard_map/dot_general | solution.py:30
  413.1 0.1 all-reduce.20.cloned.1.call-update
  413.2 0.3 all-reduce.22.cloned.1.call-start
  413.5 3.3 multiply_add_fusion.2
  416.8 0.0 copy-start.2
  416.8 51.2 %all-reduce.20.cloned.1.call-done = f32[4096,128]{1,0:T(8,128)} async-done(((f32[4096,128]{1,0:T(8,128)}), f32[4096,128]{1,0:T(8,128)}) %all-reduce.20.cloned.1.call-update) | async-done | bytes 2097168 | tf_op jit(solution)/shard_map/psum | solution.py:31
  468.0 0.0 copy-done.2
  468.0 16.7 %fusion.3 = f32[4096,128]{1,0:T(8,128)} fusion(bf16[4096,4096]{1,0:T(8,128)(2,1)} %param.5, f32[4096,128]{1,0:T(8,128)S(1)} %multiply_add_fusion.2, f32[4096,128]{1,0:T(8,128)} %all-reduce.20.cloned.1.call-done, f32[128]{0:T(128)S(1)} %copy-done.4, f32[4096]{0:T(1024)S(1)} %copy-done.3), kind=kOutput, calls=%fused_computation.9 | convolution fusion | flops 4298637312 | bytes 39862784 | tf_op jit(solution)/shard_map/dot_general | solution.py:24
  484.8 0.0 copy-start.1
  484.8 0.1 all-reduce.22.cloned.1.call-update
  484.8 0.1 all-reduce.24.cloned.1.call-start
  484.9 58.6 %all-reduce.22.cloned.1.call-done = f32[4096,128]{1,0:T(8,128)} async-done(((f32[4096,128]{1,0:T(8,128)}), f32[4096,128]{1,0:T(8,128)}) %all-reduce.22.cloned.1.call-update) | async-done | bytes 2097168 | tf_op jit(solution)/shard_map/psum | solution.py:34
  543.5 0.0 copy-done.1
  543.5 19.6 %convolution_bitcast_fusion = f32[4096,128]{1,0:T(8,128)} fusion(bf16[4096,4096]{1,0:T(8,128)(2,1)} %param.5, f32[4096,128]{1,0:T(8,128)S(1)} %copy-done.1, f32[4096,128]{1,0:T(8,128)} %all-reduce.22.cloned.1.call-done), kind=kOutput, calls=%fused_computation | convolution fusion | flops 4296540160 | bytes 39845888 | tf_op jit(solution)/shard_map/dot_general | solution.py:30
  563.0 0.1 all-reduce.24.cloned.1.call-update
  563.1 0.4 all-reduce.26.cloned.1.call-start
  563.5 54.5 %all-reduce.24.cloned.1.call-done = f32[4096,128]{1,0:T(8,128)} async-done(((f32[4096,128]{1,0:T(8,128)}), f32[4096,128]{1,0:T(8,128)}) %all-reduce.24.cloned.1.call-update) | async-done | bytes 2097168 | tf_op jit(solution)/shard_map/psum | solution.py:31
  618.0 18.0 %fusion.1 = f32[4096,128]{1,0:T(8,128)} fusion(bf16[4096,4096]{1,0:T(8,128)(2,1)} %param.5, f32[4096,128]{1,0:T(8,128)} %all-reduce.24.cloned.1.call-done, f32[128]{0:T(128)S(1)} %copy-done.4, f32[4096]{0:T(1024)S(1)} %copy-done.3, f32[4096,128]{1,0:T(8,128)} %copy-done.2, f32[4096,128]{1,0:T(8,128)} %all-reduce.20.cloned.1.call-done), kind=kOutput, calls=%fused_computation.6 | convolution fusion | flops 4301783040 | bytes 41959936 | tf_op jit(solution)/shard_map/dot_general | solution.py:24
  636.0 0.1 all-reduce.26.cloned.1.call-update
  636.0 4.2 multiply_add_fusion
  640.3 54.3 %all-reduce.26.cloned.1.call-done = f32[4096,128]{1,0:T(8,128)} async-done(((f32[4096,128]{1,0:T(8,128)}), f32[4096,128]{1,0:T(8,128)}) %all-reduce.26.cloned.1.call-update) | async-done | bytes 2097168 | tf_op jit(solution)/shard_map/psum | solution.py:34
  694.6 3.8 multiply_subtract_fusion
Async XLA Ops:
  7.2 79.3 %all-reduce.10.cloned.1.call-start = ((), (), s32[]{:S(2)}) async-start(), calls=%async_computation | async-start | bytes 4194304 | tf_op jit(solution)/shard_map/psum | solution.py:27
  24.0 139.0 %all-reduce.12.cloned.1.call-start = ((), (), s32[]{:S(2)}) async-start(), calls=%async_computation.1 | async-start | bytes 4194304 | tf_op jit(solution)/shard_map/psum | solution.py:31
  108.1 54.9 %copy-start.3 = (f32[4096]{0:T(1024)S(1)}, f32[4096]{0:T(1024)}, u32[]{:S(2)}) copy-start(f32[4096]{0:T(1024)} %param.8) | copy-start | bytes 49156
  108.1 54.9 %copy-start.4 = (f32[128]{0:T(128)S(1)}, f32[128]{0:T(128)}, u32[]{:S(2)}) copy-start(f32[128]{0:T(128)} %param.9) | copy-start | bytes 1540
  108.1 130.8 %all-reduce.14.cloned.1.call-start = ((), (), s32[]{:S(2)}) async-start(), calls=%async_computation.2 | async-start | bytes 4194304 | tf_op jit(solution)/shard_map/psum | solution.py:34
  180.4 133.0 %all-reduce.16.cloned.1.call-start = ((), (), s32[]{:S(2)}) async-start(), calls=%async_computation.3 | async-start | bytes 4194304 | tf_op jit(solution)/shard_map/psum | solution.py:31
  258.6 131.6 %all-reduce.18.cloned.1.call-start = ((), (), s32[]{:S(2)}) async-start(), calls=%async_computation.4 | async-start | bytes 4194304 | tf_op jit(solution)/shard_map/psum | solution.py:34
  331.5 136.5 %all-reduce.20.cloned.1.call-start = ((), (), s32[]{:S(2)}) async-start(), calls=%async_computation.5 | async-start | bytes 4194304 | tf_op jit(solution)/shard_map/psum | solution.py:31
  392.6 1.3 copy-start
  413.2 130.3 %all-reduce.22.cloned.1.call-start = ((), (), s32[]{:S(2)}) async-start(), calls=%async_computation.6 | async-start | bytes 4194304 | tf_op jit(solution)/shard_map/psum | solution.py:34
  416.8 51.2 %copy-start.2 = (f32[4096,128]{1,0:T(8,128)}, f32[4096,128]{1,0:T(8,128)S(1)}, u32[]{:S(2)}) copy-start(f32[4096,128]{1,0:T(8,128)S(1)} %multiply_add_fusion.2) | copy-start | bytes 6291460
  484.8 58.7 %copy-start.1 = (f32[4096,128]{1,0:T(8,128)S(1)}, f32[4096,128]{1,0:T(8,128)}, u32[]{:S(2)}) copy-start(f32[4096,128]{1,0:T(8,128)} %copy-done) | copy-start | bytes 6291460
  484.8 133.1 %all-reduce.24.cloned.1.call-start = ((), (), s32[]{:S(2)}) async-start(), calls=%async_computation.7 | async-start | bytes 4194304 | tf_op jit(solution)/shard_map/psum | solution.py:31
  563.1 131.5 %all-reduce.26.cloned.1.call-start = ((), (), s32[]{:S(2)}) async-start(), calls=%async_computation.8 | async-start | bytes 4194304 | tf_op jit(solution)/shard_map/psum | solution.py:34
Sparse Core Ops, SparseCore 0:
  24.1 62.3 all-reduce.9
  108.3 54.6 all-reduce.11
  180.5 58.4 all-reduce.13
  258.7 54.6 all-reduce.15
  331.6 58.4 all-reduce.17
  413.3 54.6 all-reduce.19
  484.9 58.4 all-reduce.21
  563.2 54.6 all-reduce.23
  636.2 58.4 all-reduce.25
where the time goes:
time: 713 us; the launch traced here: 705 us
  waiting for transfers between devices  508 us (71%)
  matrix products  164 us (23%)
  other arithmetic  16.3 us (2%)
  between operations  14.4 us (2%)
    psum x4, waiting for transfers between devices, local_sweeps(): lax.psum(block_product(step_delta), 'feat')  230 us
    psum x4, waiting for transfers between devices, local_sweeps(): gradient = lax.psum(part_grad, 'samp') / total_rows  215 us
    dot_general x5, matrix products, block_product(): jnp.dot(design, weights.astype(jnp.bfloat16), preferred_element_type=jnp....  86.8 us
    dot_general x4, matrix products, local_sweeps(): lax.dot_general(design, resid_cur.astype(jnp.bfloat16), (((0,), (0,)), ((...  77.4 us
    psum x1, waiting for transfers between devices, local_sweeps(): resid_cur = targets - lax.psum(block_product(coef_init), 'feat')  62.4 us
  transfers between devices with their start and end apart: 9, of which 9 were waited for; matrix products, arithmetic and copies ran while one was open for 1% of the time, Pallas kernels for 0%

commit v1 on v0

v1 whole, which is shorter than its diff:
```python
import functools

import jax
import jax.numpy as jnp
from jax import lax
from jax.experimental import pallas as pl
from jax.experimental.pallas import tpu as pltpu
from jax.sharding import PartitionSpec as P

SWEEPS = 4
STEP_WEIGHT = 0.5
CORES = 2
NT = (((1,), (1,)), ((), ()))
MESH = pl.DeviceIdType.MESH
BF16 = jnp.bfloat16
F32 = jnp.float32


def sweeps_kernel(ny, nf, x_hbm, y_hbm, w0_hbm, eta_ref, lam_ref, w_out, r_out,
                  x, st, rt, gp, yb, ub, sb, pb, xb, wt, res,
                  xsem, lsem, sib_s, sib_r, xs_s, xs_r, ys_s, ys_r,
                  xg_s, xg_r, xp_s, xp_r, yg_s, yg_r, wg_s, wg_r, rg_s, rg_r, rp_s, rp_r):
    nx = nf // CORES
    rows, feats = x.shape
    targets = wt.shape[0]
    rc = rows // nf
    rh = rc // 2
    fc = feats // ny
    fh = fc // 2
    inv_total = 1.0 / (rows * ny)

    yi = lax.axis_index("samp")
    fi = lax.axis_index("feat")
    chip = fi // CORES
    core = fi % CORES
    y_up, y_dn = (yi + 1) % ny, (yi + ny - 1) % ny
    y_op = (yi + 2) % ny
    c_up, c_dn = (chip + 1) % nx, (chip + nx - 1) % nx
    c_op = (chip + 2) % nx
    UP = {"feat": c_up * CORES + core}
    DN = {"feat": c_dn * CORES + core}
    SIB = {"feat": chip * CORES + 1 - core}
    YUP = {"samp": y_up}
    YDN = {"samp": y_dn}

    def rcopy(src, dst, ss, rs, dev):
        return pltpu.make_async_remote_copy(src_ref=src, dst_ref=dst, send_sem=ss, recv_sem=rs,
                                            device_id=dev, device_id_type=MESH)

    def lanes(start, size):
        return pl.ds(pl.multiple_of(start, 128), size)

    def srows(start, size):
        return pl.ds(pl.multiple_of(start, 128), size)

    def ring_off(j):
        return (2 + 3 * j + 3 * (j // 2) + 2 * (j // 3)) % 4

    def row_chunk(i):
        j, who = i // 2, i % 2
        d = (chip + ring_off(j)) % nx
        return d * CORES + core + (1 - who) * (1 - 2 * core)

    def xload(i):
        c = row_chunk(i)
        return pltpu.make_async_copy(x_hbm.at[srows(c * rc, rc), :], x.at[srows(c * rc, rc), :], xsem.at[i])

    w0_copy = pltpu.make_async_copy(w0_hbm, w_out, lsem.at[0])
    y_copy = pltpu.make_async_copy(y_hbm.at[srows(fi * rc, rc), :], res, lsem.at[1])
    w0_copy.start()
    for i in range(nf):
        xload(i).start()
    y_copy.start()

    barrier = pltpu.get_barrier_semaphore()
    peers = (UP, DN, SIB, YUP, YDN)
    for dev in peers:
        pl.semaphore_signal(barrier, inc=1, device_id=dev, device_id_type=MESH)

    w0_copy.wait()

    def w0_step(i, c):
        blk = w_out[srows(i * rc, rc), :]
        st[:, lanes(i * rc, rc)] = jnp.transpose(blk).astype(BF16)
        return c
    lax.fori_loop(0, feats // rc, w0_step, 0)
    for h in range(2):
        wt[:, pl.ds(h * fh, fh)] = jnp.transpose(w_out[srows(yi * fc + h * fh, fh), :])
    pl.semaphore_wait(barrier, len(peers))
    y_copy.wait()

    def sib_copy(j):
        return rcopy(ub.at[2 * j], sb.at[j], sib_s.at[j], sib_r.at[j], SIB)

    H0, H1 = pl.ds(0, rh), pl.ds(rh, rh)
    x_rs = [
        lambda: rcopy(pb.at[0, H0], xb.at[0], xs_s.at[0], xs_r.at[0], UP),
        lambda: rcopy(pb.at[0, H1], xb.at[1], xs_s.at[1], xs_r.at[1], DN),
        lambda: rcopy(pb.at[1, H1], xb.at[2], xs_s.at[2], xs_r.at[2], UP),
        lambda: rcopy(pb.at[2, H0], xb.at[3], xs_s.at[3], xs_r.at[3], DN),
        lambda: rcopy(pb.at[1, H0], xb.at[4], xs_s.at[4], xs_r.at[4], UP),
        lambda: rcopy(pb.at[2, H1], xb.at[5], xs_s.at[5], xs_r.at[5], DN),
    ]

    def gsl(d, h):
        return gp.at[:, lanes(d * fc + h * fh, fh)]
    y_rs = [
        lambda: rcopy(gsl(y_op, 0), yb.at[0], ys_s.at[0], ys_r.at[0], YUP),
        lambda: rcopy(gsl(y_op, 1), yb.at[1], ys_s.at[1], ys_r.at[1], YDN),
        lambda: rcopy(gsl(y_up, 1), yb.at[2], ys_s.at[2], ys_r.at[2], YUP),
        lambda: rcopy(gsl(y_dn, 0), yb.at[3], ys_s.at[3], ys_r.at[3], YDN),
        lambda: rcopy(gsl(y_up, 0), yb.at[4], ys_s.at[4], ys_r.at[4], YUP),
        lambda: rcopy(gsl(y_dn, 1), yb.at[5], ys_s.at[5], ys_r.at[5], YDN),
    ]

    def gather(piece, ss, rs, up, dn, me, below, above):
        return [
            lambda: rcopy(piece(me, 0), piece(me, 0), ss.at[0], rs.at[0], up),
            lambda: rcopy(piece(me, 1), piece(me, 1), ss.at[1], rs.at[1], up),
            lambda: rcopy(piece(me, 0), piece(me, 0), ss.at[2], rs.at[2], dn),
            lambda: rcopy(piece(me, 1), piece(me, 1), ss.at[3], rs.at[3], dn),
            lambda: rcopy(piece(below, 0), piece(below, 0), ss.at[4], rs.at[4], up),
            lambda: rcopy(piece(above, 1), piece(above, 1), ss.at[5], rs.at[5], dn),
        ]

    y_ag = gather(lambda d, h: st.at[:, lanes(d * fc + h * fh, fh)], yg_s, yg_r, YUP, YDN, yi, y_dn, y_up)
    x_ag = gather(lambda d, h: rt.at[:, lanes((d * CORES + core) * rc + h * rh, rh)], xg_s, xg_r, UP, DN, chip, c_dn, c_up)
    w_ag = gather(lambda d, h: w_out.at[srows(d * fc + h * fh, fh), :], wg_s, wg_r, YUP, YDN, yi, y_dn, y_up)
    r_ag = gather(lambda d, h: r_out.at[srows((d * CORES + core) * rc + h * rh, rh), :], rg_s, rg_r, UP, DN, chip, c_dn, c_up)

    def pair(piece, half, ss, rs):
        return [
            lambda: rcopy(piece(chip), piece(chip), ss.at[0], rs.at[0], SIB),
            lambda: rcopy(piece(c_dn), piece(c_dn), ss.at[1], rs.at[1], SIB),
            lambda: rcopy(piece(c_up), piece(c_up), ss.at[2], rs.at[2], SIB),
            lambda: rcopy(half(c_op, 0), half(c_op, 0), ss.at[3], rs.at[3], SIB),
            lambda: rcopy(half(c_op, 1), half(c_op, 1), ss.at[4], rs.at[4], SIB),
        ]
    x_pair = pair(lambda d: rt.at[:, lanes((d * CORES + core) * rc, rc)],
                  lambda d, h: rt.at[:, lanes((d * CORES + core) * rc + h * rh, rh)], xp_s, xp_r)
    r_pair = pair(lambda d: r_out.at[srows((d * CORES + core) * rc, rc), :],
                  lambda d, h: r_out.at[srows((d * CORES + core) * rc + h * rh, rh), :], rp_s, rp_r)

    def ring_and_pair(ag, pr):
        ag[0]().wait_recv()
        ag[4]().start()
        ag[3]().wait_recv()
        ag[5]().start()
        ag[1]().wait_recv()
        pr[1]().start()
        ag[2]().wait_recv()
        pr[2]().start()
        ag[4]().wait_recv()
        pr[3]().start()
        ag[5]().wait_recv()
        pr[4]().start()
        for c in pr:
            c().wait_recv()

    def sweep(k, carry):
        def u_step(i, c):
            j, who = i // 2, i % 2

            @pl.when(k == 0)
            def _():
                xload(i).wait()
            u = lax.dot_general(x[srows(row_chunk(i) * rc, rc), :], st[...], NT, preferred_element_type=F32)
            ub[i] = u.astype(BF16)

            @pl.when(who == 0)
            def _():
                sib_copy(j).start()

            @pl.when(who == 1)
            def _():
                sib_copy(j).wait_recv()
                pb[j] = ub[i].astype(F32) + sb[j].astype(F32)

            @pl.when(i == 1)
            def _():
                x_rs[0]().start()
                x_rs[1]().start()

            @pl.when(i == 3)
            def _():
                x_rs[2]().start()

            @pl.when(i == 5)
            def _():
                x_rs[3]().start()
                x_rs[0]().wait_recv()
                pb[1, H0] = pb[1, H0] + xb[0]
                x_rs[4]().start()
                x_rs[1]().wait_recv()
                pb[2, H1] = pb[2, H1] + xb[1]
                x_rs[5]().start()
            return c
        lax.fori_loop(0, nf, u_step, 0)

        scale = jnp.where(k == 0, 1.0, STEP_WEIGHT).astype(F32)
        x_rs[3]().wait_recv()
        x_rs[4]().wait_recv()
        res[H0] = res[H0] - scale * (pb[3, H0] + xb[3] + xb[4])
        x_rs[2]().wait_recv()
        x_rs[5]().wait_recv()
        res[H1] = res[H1] - scale * (pb[3, H1] + xb[2] + xb[5])

        @pl.when(k < SWEEPS)
        def _():
            rt[:, lanes(fi * rc, rh)] = jnp.transpose(res[H0]).astype(BF16)
            x_ag[0]().start()
            x_ag[2]().start()
            rt[:, lanes(fi * rc + rh, rh)] = jnp.transpose(res[H1]).astype(BF16)
            x_ag[3]().start()
            x_ag[1]().start()
            x_pair[0]().start()
            for j in range(nx):
                sib_copy(j).wait_send()
            for c in x_rs:
                c().wait_send()
            ring_and_pair(x_ag, x_pair)

            def g_step(i, c):
                j, h = i // 2, i % 2
                col = lanes(((yi + ring_off(j)) % ny) * fc + h * fh, fh)
                gp[:, col] = jnp.dot(rt[...], x[:, col], preferred_element_type=F32)
                for step, n in ((0, 0), (1, 1), (3, 2), (4, 3)):
                    @pl.when(i == step)
                    def _():
                        y_rs[n]().start()
                return c
            lax.fori_loop(0, 2 * ny, g_step, 0)
            for c in x_ag + x_pair:
                c().wait_send()
            y_rs[0]().wait_recv()
            up0 = lanes(y_up * fc, fh)
            gp[:, up0] = gp[:, up0] + yb[0]
            y_rs[4]().start()
            y_rs[1]().wait_recv()
            dn1 = lanes(y_dn * fc + fh, fh)
            gp[:, dn1] = gp[:, dn1] + yb[1]
            y_rs[5]().start()

            def s_half(h, a, b):
                own = lanes(yi * fc + h * fh, fh)
                wsl = pl.ds(h * fh, fh)
                g = (gp[:, own] + yb[a] + yb[b]) * inv_total
                w = wt[:, wsl]
                s = eta_ref[:, own] * (g - lam_ref[...] * w)
                wt[:, wsl] = w + STEP_WEIGHT * s
                st[:, own] = s.astype(BF16)

            y_rs[3]().wait_recv()
            y_rs[4]().wait_recv()
            s_half(0, 3, 4)
            y_ag[0]().start()
            y_rs[2]().wait_recv()
            y_rs[5]().wait_recv()
            s_half(1, 2, 5)
            y_ag[3]().start()
            y_ag[1]().start()
            y_ag[2]().start()
            for c in y_rs:
                c().wait_send()

            @pl.when(k == SWEEPS - 1)
            def _():
                for h in range(2):
                    w_out[srows(yi * fc + h * fh, fh), :] = jnp.transpose(wt[:, pl.ds(h * fh, fh)])
            y_ag[0]().wait_recv()
            y_ag[4]().start()
            y_ag[3]().wait_recv()
            y_ag[5]().start()
            for n in (1, 2, 4, 5):
                y_ag[n]().wait_recv()

            @pl.when(k == SWEEPS - 1)
            def _():
                for n in (0, 3, 1, 2):
                    w_ag[n]().start()
            for c in y_ag:
                c().wait_send()
        return carry

    lax.fori_loop(0, SWEEPS + 1, sweep, 0)

    r_out[srows(fi * rc, rc), :] = res[...]
    for n in (0, 3, 1, 2):
        r_ag[n]().start()
    r_pair[0]().start()
    w_ag[0]().wait_recv()
    w_ag[4]().start()
    w_ag[3]().wait_recv()
    w_ag[5]().start()
    for j in range(nx):
        sib_copy(j).wait_send()
    for c in x_rs:
        c().wait_send()
    ring_and_pair(r_ag, r_pair)
    for n in (1, 2, 4, 5):
        w_ag[n]().wait_recv()
    for c in w_ag + r_ag + r_pair:
        c().wait_send()


def solution(mesh):
    ny, nf = mesh.shape["samp"], mesh.shape["feat"]
    design_spec = P(("problem", "samp"), "feat")
    rows_spec = P(("problem", "samp"), None)
    coef_spec = P(("problem", "feat"), None)
    step_spec = P(("problem", "feat"))
    ridge_spec = P("problem")

    def local_sweeps(design, targets, coef_init, step_sizes, ridge_weights):
        rows, feats = design.shape
        nt = targets.shape[1]
        rc, fc = rows // nf, feats // ny
        nx = nf // CORES
        dma = lambda n: pltpu.SemaphoreType.DMA((n,))
        anyspec = pl.BlockSpec(memory_space=pl.ANY)
        vspec = pl.BlockSpec(memory_space=pltpu.VMEM)
        return pl.pallas_call(
            functools.partial(sweeps_kernel, ny, nf),
            out_shape=(jax.ShapeDtypeStruct((feats, nt), F32), jax.ShapeDtypeStruct((rows, nt), F32)),
            in_specs=[anyspec, anyspec, anyspec, vspec, vspec],
            out_specs=(vspec, vspec),
            scratch_shapes=[
                pltpu.VMEM((rows, feats), BF16),
                pltpu.VMEM((nt, feats), BF16),
                pltpu.VMEM((nt, rows), BF16),
                pltpu.VMEM((nt, feats), F32),
                pltpu.VMEM((6, nt, fc // 2), F32),
                pltpu.VMEM((nf, rc, nt), BF16),
                pltpu.VMEM((nx, rc, nt), BF16),
                pltpu.VMEM((nx, rc, nt), F32),
                pltpu.VMEM((6, rc // 2, nt), F32),
                pltpu.VMEM((nt, fc), F32),
                pltpu.VMEM((rc, nt), F32),
                dma(nf), dma(2), dma(nx), dma(nx), dma(6), dma(6), dma(6), dma(6),
                dma(6), dma(6), dma(5), dma(5), dma(6), dma(6), dma(6), dma(6), dma(6), dma(6), dma(5), dma(5),
            ],
            compiler_params=pltpu.CompilerParams(
                collective_id=0, has_side_effects=True, vmem_limit_bytes=60 * 1024 * 1024),
            name="sweeps",
        )(design, targets, coef_init, step_sizes[None, :], ridge_weights[:, None])

    return jax.shard_map(local_sweeps, mesh=mesh, in_specs=(design_spec, rows_spec, coef_spec, step_spec, ridge_spec),
                         out_specs=(coef_spec, rows_spec), check_vma=False)
```

time: 713 us -> 272 us (0.38); the launches traced: 705 us -> 272 us
  waiting for transfers between devices: 508 us -> 0 us
  Pallas kernels: 0 us -> 266 us
  matrix products: 164 us -> 0 us
  other arithmetic: 16.3 us -> 0 us
  between operations: 14.4 us -> 0.65 us
    psum x9 -> x0, waiting for transfers between devices: 507 us -> none  [the longest x4 230 us: local_sweeps(): lax.psum(block_product(step_delta), 'feat')]
    pallas_call x0 -> x1, Pallas kernels: none -> 266 us  [local_sweeps(): pl.pallas_call(functools.partial(sweeps_kernel, ny, nf), out_shape=(jax.S...]
    dot_general x9 -> x0, matrix products: 164 us -> none  [the longest x5 86.8 us: block_product(): jnp.dot(design, weights.astype(jnp.bfloat16), preferred_element_type=jnp....]
    sub x3 -> x0, other arithmetic: 8.74 us -> none  [the longest x2 6.31 us: local_sweeps(): resid_cur - STEP_WEIGHT * lax.psum(block_product(step_delta), 'feat')]
    add x2 -> x0, other arithmetic: 7.53 us -> none  [local_sweeps(): coef_cur = coef_cur + STEP_WEIGHT * step_delta]
  transfers between devices with their start and end apart: 9 -> 0, of which waited for: 9 -> 0; matrix products, arithmetic and copies ran while one was open for 1% -> 0% of each run, Pallas kernels for 0% -> 0%
where the time goes in v1:
time: 272 us
  Pallas kernels  266 us (98%)
  local copies, waits for them, and re-layouts  5.91 us (2%)
    pallas_call x1, Pallas kernels, local_sweeps(): pl.pallas_call(functools.partial(sweeps_kernel, ny, nf), out_shape=(jax.S...  266 us

profile of v1, /device:TPU:97, one launch (start us, length us, event | category | flops | bytes accessed | tf_op | source)
XLA Modules:
  0.0 272.3 jit_solution(10757247702372544039)
XLA Ops:
  0.6 1.4 copy.7.lam_ref
  2.0 265.8 %sweeps.1 = (f32[4096,128]{1,0:T(8,128)}, f32[4096,128]{1,0:T(8,128)}) custom-call(bf16[4096,4096]{1,0:T(8,128)(2,1)} %x_hbm.1, f32[4096,128]{1,0:T(8,128)} %y_hbm.1, f32[4096,128]{1,0:T(8,128)} %w0_hbm.1, f32[1,4096]{1,0:T(1,128)} %bitcast.2, f32[128,1]{1,0:T(8,128)} %copy.7.lam_ref), custom_call_target="tpu_custom_call" | custom-call | tf_op jit(solution)/shard_map/sweeps/pallas_call | solution.py:322
  267.8 0.0 copy-start
  267.8 3.2 %copy.10 = f32[4096,128]{1,0:T(8,128)} copy(f32[4096,128]{1,0:T(8,128)} %get-tuple-element.4) | data formatting | bytes 4194304
  271.0 0.0 copy-done
  271.0 1.3 copy.11
Async XLA Ops:
  267.8 3.2 %copy-start = (f32[4096,128]{1,0:T(8,128)S(1)}, f32[4096,128]{1,0:T(8,128)}, u32[]{:S(2)}) copy-start(f32[4096,128]{1,0:T(8,128)} %get-tuple-element.5) | copy-start | bytes 6291460

commit v2 on v0

v2 whole, which is shorter than its diff:
```python
import functools

import jax
import jax.numpy as jnp
from jax import lax
from jax.experimental import pallas as pl
from jax.experimental.pallas import tpu as pltpu
from jax.sharding import PartitionSpec as P

SWEEPS = 4
STEP_WEIGHT = 0.5
CORES = 2
NT = (((1,), (1,)), ((), ()))
MESH = pl.DeviceIdType.MESH
BF16 = jnp.bfloat16
F32 = jnp.float32


def sweeps_kernel(ny, nf, x_hbm, y_hbm, w0_hbm, eta_ref, lam_ref, w_out, r_out,
                  x, st, rt, gp, yb, ub, sb, pb, xb, wt, res, ua, w0b, lam_col,
                  xsem, lsem, sib_s, sib_r, xs_s, xs_r, ys_s, ys_r,
                  xg_s, xg_r, xp_s, xp_r, yg_s, yg_r, wg_s, wg_r, rg_s, rg_r, rp_s, rp_r):
    nx = nf // CORES
    rows, feats = x.shape
    targets = wt.shape[0]
    rc = rows // nf
    rh = rc // 2
    fc = feats // ny
    fh = fc // 2
    inv_total = 1.0 / (rows * ny)

    yi = lax.axis_index("samp")
    fi = lax.axis_index("feat")
    chip = fi // CORES
    core = fi % CORES
    y_up, y_dn = (yi + 1) % ny, (yi + ny - 1) % ny
    y_op = (yi + 2) % ny
    c_up, c_dn = (chip + 1) % nx, (chip + nx - 1) % nx
    c_op = (chip + 2) % nx
    UP = {"feat": c_up * CORES + core}
    DN = {"feat": c_dn * CORES + core}
    SIB = {"feat": chip * CORES + 1 - core}
    YUP = {"samp": y_up}
    YDN = {"samp": y_dn}

    def rcopy(src, dst, ss, rs, dev):
        return pltpu.make_async_remote_copy(src_ref=src, dst_ref=dst, send_sem=ss, recv_sem=rs,
                                            device_id=dev, device_id_type=MESH)

    def lanes(start, size):
        return pl.ds(pl.multiple_of(start, 128), size)

    def srows(start, size):
        return pl.ds(pl.multiple_of(start, 128), size)

    def ring_off(j):
        return (2 + 3 * j + 3 * (j // 2) + 2 * (j // 3)) % 4

    def row_chunk(i):
        j, who = i // 2, i % 2
        d = (chip + ring_off(j)) % nx
        return d * CORES + core + (1 - who) * (1 - 2 * core)

    def xload(i):
        c = row_chunk(i)
        return pltpu.make_async_copy(x_hbm.at[srows(c * rc, rc), :], x.at[srows(c * rc, rc), :], xsem.at[i])

    w0_copy = pltpu.make_async_copy(w0_hbm, w_out, lsem.at[0])
    y_copy = pltpu.make_async_copy(y_hbm.at[srows(fi * rc, rc), :], res, lsem.at[1])
    w0_copy.start()
    for i in range(1):
        xload(i).start()
    y_copy.start()

    barrier = pltpu.get_barrier_semaphore()
    peers = (UP, DN, SIB, YUP, YDN)
    for dev in peers:
        pl.semaphore_signal(barrier, inc=1, device_id=dev, device_id_type=MESH)

    w0_copy.wait()
    for i in range(1, 3):
        xload(i).start()

    w0b[...] = w_out[...].astype(BF16)
    lam_col[...] = jnp.transpose(jnp.broadcast_to(lam_ref[...], (lam_col.shape[1], targets)))
    for h in range(2):
        wt[:, pl.ds(h * fh, fh)] = jnp.transpose(w_out[srows(yi * fc + h * fh, fh), :])
    pl.semaphore_wait(barrier, len(peers))
    y_copy.wait()

    PIECES = range(2)
    rq, fq = rc // 4, fc // 4

    def wait_sends(copies):
        for c in copies:
            c.wait_send()

    def sib_copy(j):
        return rcopy(ub.at[2 * j], sb.at[j], sib_s.at[j], sib_r.at[j], SIB)

    def rpos(p, h):
        return pl.ds(p * rh + h * rq, rq)

    def x_rs(p, n):
        j, h = ((0, 0), (0, 1), (1, 1), (2, 0), (1, 0), (2, 1))[n]
        return rcopy(pb.at[j, rpos(p, h)], xb.at[6 * p + n], xs_s.at[6 * p + n], xs_r.at[6 * p + n], (UP, DN)[n % 2])

    def gpos(d, p, h):
        return lanes(d * fc + p * fh + h * fq, fq)

    def y_rs(p, n):
        d, h = ((y_op, 0), (y_op, 1), (y_up, 1), (y_dn, 0), (y_up, 0), (y_dn, 1))[n]
        return rcopy(gp.at[:, gpos(d, p, h)], yb.at[6 * p + n], ys_s.at[6 * p + n], ys_r.at[6 * p + n], (YUP, YDN)[n % 2])

    def ring(at, ss, rs, up, dn, me, below, above):
        def copy(p, n):
            d, h = ((me, 0), (me, 1), (me, 1), (me, 0), (below, 0), (above, 1))[n]
            src = at(d, p, h)
            return rcopy(src, src, ss.at[6 * p + n], rs.at[6 * p + n], (up, dn)[n % 2])
        return copy

    def xpos(d, p, h):
        return (d * CORES + core) * rc + p * rh + h * rq

    def wpos(d, p, h):
        return srows(d * fc + p * fh + h * fq, fq)

    y_ag = ring(lambda d, p, h: st.at[:, gpos(d, p, h)], yg_s, yg_r, YUP, YDN, yi, y_dn, y_up)
    x_ag = ring(lambda d, p, h: rt.at[:, lanes(xpos(d, p, h), rq)], xg_s, xg_r, UP, DN, chip, c_dn, c_up)
    w_ag = ring(lambda d, p, h: w_out.at[wpos(d, p, h), :], wg_s, wg_r, YUP, YDN, yi, y_dn, y_up)
    r_ag = ring(lambda d, p, h: r_out.at[srows(xpos(d, p, h), rq), :], rg_s, rg_r, UP, DN, chip, c_dn, c_up)

    def pair(at, ss, rs):
        def copy(p, n):
            d, h, size = ((chip, 0, rh), (c_dn, 0, rh), (c_up, 0, rh), (c_op, 0, rq), (c_op, 1, rq))[n]
            src = at(xpos(d, p, h), size)
            return rcopy(src, src, ss.at[5 * p + n], rs.at[5 * p + n], SIB)
        return copy

    x_pair = pair(lambda o, n: rt.at[:, lanes(o, n)], xp_s, xp_r)
    r_pair = pair(lambda o, n: r_out.at[srows(o, n), :], rp_s, rp_r)

    def all_of(copy, n):
        return [copy(p, i) for p in PIECES for i in range(n)]

    def start_own(ag, p):
        for n in range(4):
            ag(p, n).start()

    def pass_on(ag, p):
        for n in range(2):
            ag(p, n).wait_recv()
            ag(p, n + 4).start()

    def ring_and_pair(ag, pr):
        for p in PIECES:
            pass_on(ag, p)
            ag(p, 2).wait_recv()
            pr(p, 1).start()
            ag(p, 3).wait_recv()
            pr(p, 2).start()
        for p in PIECES:
            for n in range(2):
                ag(p, n + 4).wait_recv()
                pr(p, n + 3).start()
        for c in all_of(pr, 5):
            c.wait_recv()

    def combine():
        for p in PIECES:
            for n, j in ((0, 1), (1, 2)):
                x_rs(p, n).wait_recv()
                sl = rpos(p, n)
                pb[j, sl] = pb[j, sl] + xb[6 * p + n]
                x_rs(p, n + 4).start()

    def send_sums(j):
        for p in PIECES:
            for n in ((0, 1), (2,), (3,), ())[j]:
                x_rs(p, n).start()

    def scatter_first():
        def step(i, c):
            j, who = i // 2, i % 2
            ub[i] = first_product(i).astype(BF16)

            @pl.when(who == 0)
            def _():
                sib_copy(j).start()

            @pl.when(who == 1)
            def _():
                sib_copy(j).wait_recv()
                pb[j] = ub[i].astype(F32) + sb[j].astype(F32)
            for jj in range(3):
                @pl.when(i == 2 * jj + 1)
                def _():
                    send_sums(jj)

            @pl.when(i == 5)
            def _():
                combine()
            return c
        lax.fori_loop(0, nf, step, 0)

    def scatter_last():
        for i in (0, 2, 4, 1, 6, 3, 5, 7):
            j, who = i // 2, i % 2
            u = last_product(i).astype(BF16)
            if who == 0:
                ub[i] = u
                sib_copy(j).start()
            else:
                sib_copy(j).wait_recv()
                pb[j] = u.astype(F32) + sb[j].astype(F32)
                send_sums(j)
        combine()

    def finish_piece(p, scale):
        for h, a, b in ((0, 3, 4), (1, 2, 5)):
            x_rs(p, a).wait_recv()
            x_rs(p, b).wait_recv()
            sl = rpos(p, h)
            res[sl] = res[sl] - scale * (pb[3, sl] + xb[6 * p + a] + xb[6 * p + b])

    def first_product(i):
        xload(i).wait()

        @pl.when(i + 3 < nf)
        def _():
            xload(i + 3).start()
        return jnp.dot(x[srows(row_chunk(i) * rc, rc), :], w0b[...], preferred_element_type=F32)

    def part(d, p, first):
        nb = 2
        step = rows // nb

        def body(i, c):
            rs = srows(i * step, step)
            cs = lanes(d * fc + p * fh, fh)
            v = lax.dot_general(x[rs, cs], st[:, cs], NT, preferred_element_type=F32)
            ua[rs, :] = v if first else ua[rs, :] + v
            return c
        lax.fori_loop(0, nb, body, 0)

    def last_product(i):
        rs = srows(row_chunk(i) * rc, rc)
        cs = lanes(y_op * fc, fc)
        return ua[rs, :] + lax.dot_general(x[rs, cs], st[:, cs], NT, preferred_element_type=F32)

    def sweep(k, carry):
        scale = jnp.where(k == 0, 1.0, STEP_WEIGHT).astype(F32)
        for p in PIECES:
            finish_piece(p, scale)
            rt[:, lanes(fi * rc + p * rh, rh)] = jnp.transpose(res[pl.ds(p * rh, rh)]).astype(BF16)
            start_own(x_ag, p)
            x_pair(p, 0).start()
        wait_sends([sib_copy(j) for j in range(nx)])
        wait_sends(all_of(x_rs, 6))
        ring_and_pair(x_ag, x_pair)

        def g_step(i, c):
            j, q = i // 2, i % 2
            col = lanes(((yi + ring_off(j)) % ny) * fc + q * fh, fh)
            gp[:, col] = jnp.dot(rt[...], x[:, col], preferred_element_type=F32)
            for p in PIECES:
                for jj, ns in ((0, (0, 1)), (1, (2,)), (2, (3,))):
                    @pl.when(i == 2 * jj + p)
                    def _():
                        for n in ns:
                            y_rs(p, n).start()
            return c
        lax.fori_loop(0, 2 * ny, g_step, 0)
        wait_sends(all_of(x_ag, 6) + all_of(x_pair, 5))
        for p in PIECES:
            for n, d in ((0, y_up), (1, y_dn)):
                y_rs(p, n).wait_recv()
                col = gpos(d, p, n)
                gp[:, col] = gp[:, col] + yb[6 * p + n]
                y_rs(p, n + 4).start()

        for p in PIECES:
            for h, a, b in ((0, 3, 4), (1, 2, 5)):
                y_rs(p, a).wait_recv()
                y_rs(p, b).wait_recv()
                own = gpos(yi, p, h)
                wsl = pl.ds(p * fh + h * fq, fq)
                g = (gp[:, own] + yb[6 * p + a] + yb[6 * p + b]) * inv_total
                w = wt[:, wsl]
                s = eta_ref[:, own] * (g - lam_col[...] * w)
                wt[:, wsl] = w + STEP_WEIGHT * s
                st[:, own] = s.astype(BF16)
            start_own(y_ag, p)
            part(yi, p, p == 0)
        pass_on(y_ag, 0)
        for n in (2, 3):
            y_ag(0, n).wait_recv()
        part(y_dn, 0, False)
        pass_on(y_ag, 1)
        part(y_up, 0, False)
        for n in (2, 3):
            y_ag(1, n).wait_recv()
        part(y_dn, 1, False)
        part(y_up, 1, False)
        wait_sends(all_of(y_rs, 6))

        @pl.when(k == SWEEPS - 1)
        def _():
            w_out[srows(yi * fc, fc), :] = jnp.transpose(wt[...])
        for p in PIECES:
            for n in (4, 5):
                y_ag(p, n).wait_recv()

        @pl.when(k == SWEEPS - 1)
        def _():
            for p in PIECES:
                start_own(w_ag, p)
        scatter_last()
        wait_sends(all_of(y_ag, 6))
        return carry

    scatter_first()
    lax.fori_loop(0, SWEEPS, sweep, 0)

    for p in PIECES:
        finish_piece(p, STEP_WEIGHT)
        r_out[srows(fi * rc + p * rh, rh), :] = res[pl.ds(p * rh, rh)]
        start_own(r_ag, p)
        r_pair(p, 0).start()
    for p in PIECES:
        pass_on(w_ag, p)
    wait_sends([sib_copy(j) for j in range(nx)])
    wait_sends(all_of(x_rs, 6))

    ring_and_pair(r_ag, r_pair)
    for p in PIECES:
        for n in range(2, 6):
            w_ag(p, n).wait_recv()
    wait_sends(all_of(w_ag, 6) + all_of(r_ag, 6) + all_of(r_pair, 5))


def solution(mesh):
    ny, nf = mesh.shape["samp"], mesh.shape["feat"]
    design_spec = P(("problem", "samp"), "feat")
    rows_spec = P(("problem", "samp"), None)
    coef_spec = P(("problem", "feat"), None)
    step_spec = P(("problem", "feat"))
    ridge_spec = P("problem")

    def local_sweeps(design, targets, coef_init, step_sizes, ridge_weights):
        rows, feats = design.shape
        nt = targets.shape[1]
        rc, fc = rows // nf, feats // ny
        nx = nf // CORES
        dma = lambda n: pltpu.SemaphoreType.DMA((n,))
        anyspec = pl.BlockSpec(memory_space=pl.ANY)
        vspec = pl.BlockSpec(memory_space=pltpu.VMEM)
        return pl.pallas_call(
            functools.partial(sweeps_kernel, ny, nf),
            out_shape=(pltpu.VMEM((feats, nt), F32), pltpu.VMEM((rows, nt), F32)),
            in_specs=[anyspec, anyspec, anyspec, vspec, vspec],
            out_specs=(vspec, vspec),
            scratch_shapes=[
                pltpu.VMEM((rows, feats), BF16),
                pltpu.VMEM((nt, feats), BF16),
                pltpu.VMEM((nt, rows), BF16),
                pltpu.VMEM((nt, feats), F32),
                pltpu.VMEM((12, nt, fc // 4), F32),
                pltpu.VMEM((nf, rc, nt), BF16),
                pltpu.VMEM((nx, rc, nt), BF16),
                pltpu.VMEM((nx, rc, nt), F32),
                pltpu.VMEM((12, rc // 4, nt), F32),
                pltpu.VMEM((nt, fc), F32),
                pltpu.VMEM((rc, nt), F32),
                pltpu.VMEM((rows, nt), F32),
                pltpu.VMEM((feats, nt), BF16),
                pltpu.VMEM((nt, fc // 4), F32),
                dma(nf), dma(2), dma(nx), dma(nx), dma(12), dma(12), dma(12), dma(12),
                dma(12), dma(12), dma(10), dma(10), dma(12), dma(12), dma(12), dma(12), dma(12), dma(12), dma(10), dma(10),
            ],
            compiler_params=pltpu.CompilerParams(
                collective_id=0, has_side_effects=True, vmem_limit_bytes=54 * 1024 * 1024),
            name="sweeps",
        )(design, targets, coef_init, step_sizes[None, :], ridge_weights[None, :])
    return jax.shard_map(local_sweeps, mesh=mesh, in_specs=(design_spec, rows_spec, coef_spec, step_spec, ridge_spec),
                         out_specs=(coef_spec, rows_spec), check_vma=False)
```

time: 713 us -> 240 us (0.34); the launches traced: 705 us -> 240 us
  waiting for transfers between devices: 508 us -> 0 us
  Pallas kernels: 0 us -> 237 us
  matrix products: 164 us -> 0 us
  other arithmetic: 16.3 us -> 0 us
  between operations: 14.4 us -> 0.64 us
    psum x9 -> x0, waiting for transfers between devices: 507 us -> none  [the longest x4 230 us: local_sweeps(): lax.psum(block_product(step_delta), 'feat')]
    pallas_call x0 -> x1, Pallas kernels: none -> 237 us  [local_sweeps(): pl.pallas_call(functools.partial(sweeps_kernel, ny, nf), out_shape=(pltpu...]
    dot_general x9 -> x0, matrix products: 164 us -> none  [the longest x5 86.8 us: block_product(): jnp.dot(design, weights.astype(jnp.bfloat16), preferred_element_type=jnp....]
    sub x3 -> x0, other arithmetic: 8.74 us -> none  [the longest x2 6.31 us: local_sweeps(): resid_cur - STEP_WEIGHT * lax.psum(block_product(step_delta), 'feat')]
    add x2 -> x0, other arithmetic: 7.53 us -> none  [local_sweeps(): coef_cur = coef_cur + STEP_WEIGHT * step_delta]
  transfers between devices with their start and end apart: 9 -> 0, of which waited for: 9 -> 0; matrix products, arithmetic and copies ran while one was open for 1% -> 0% of each run, Pallas kernels for 0% -> 0%
where the time goes in v2:
time: 240 us
  Pallas kernels  237 us (99%)
  local copies, waits for them, and re-layouts  2.64 us (1%)
    pallas_call x1, Pallas kernels, local_sweeps(): pl.pallas_call(functools.partial(sweeps_kernel, ny, nf), out_shape=(pltpu...  237 us

profile of v2, /device:TPU:97, one launch (start us, length us, event | category | flops | bytes accessed | tf_op | source)
XLA Modules:
  0.0 240.0 jit_solution(13250012985844459775)
XLA Ops:
  0.6 236.8 %sweeps.1 = (f32[4096,128]{1,0:T(8,128)S(1)}, f32[4096,128]{1,0:T(8,128)S(1)}) custom-call(bf16[4096,4096]{1,0:T(8,128)(2,1)} %x_hbm.1, f32[4096,128]{1,0:T(8,128)} %y_hbm.1, f32[4096,128]{1,0:T(8,128)} %w0_hbm.1, f32[1,4096]{1,0:T(1,128)} %bitcast.2, f32[1,128]{1,0:T(1,128)} %bitcast.3), custom_call_target="tpu_custom_call" | custom-call | tf_op jit(solution)/shard_map/sweeps/pallas_call | solution.py:358
  237.4 1.3 copy.9
  238.7 1.3 copy.10

commit v3 on v2

--- a/solution.py
+++ b/solution.py
@@ -40,6 +40,8 @@
     UP = {"feat": c_up * CORES + core}
     DN = {"feat": c_dn * CORES + core}
     SIB = {"feat": chip * CORES + 1 - core}
+    UPX = {"feat": c_up * CORES + 1 - core}
+    DNX = {"feat": c_dn * CORES + 1 - core}
     YUP = {"samp": y_up}
     YDN = {"samp": y_dn}
 
@@ -52,6 +54,9 @@
 
     def srows(start, size):
         return pl.ds(pl.multiple_of(start, 128), size)
+
+    def erows(start, size):
+        return pl.ds(pl.multiple_of(start, 8), size)
 
     def ring_off(j):
         return (2 + 3 * j + 3 * (j // 2) + 2 * (j // 3)) % 4
@@ -73,7 +78,7 @@
     y_copy.start()
 
     barrier = pltpu.get_barrier_semaphore()
-    peers = (UP, DN, SIB, YUP, YDN)
+    peers = (UP, DN, UPX, DNX, SIB, YUP, YDN)
     for dev in peers:
         pl.semaphore_signal(barrier, inc=1, device_id=dev, device_id_type=MESH)
 
@@ -82,18 +87,20 @@
         xload(i).start()
 
     w0b[...] = w_out[...].astype(BF16)
-    lam_col[...] = jnp.transpose(jnp.broadcast_to(lam_ref[...], (lam_col.shape[1], targets)))
-    for h in range(2):
-        wt[:, pl.ds(h * fh, fh)] = jnp.transpose(w_out[srows(yi * fc + h * fh, fh), :])
     pl.semaphore_wait(barrier, len(peers))
-    y_copy.wait()
 
     PIECES = range(2)
+    FINE = range(4)
     rq, fq = rc // 4, fc // 4
+    re = rc // 4
 
     def wait_sends(copies):
         for c in copies:
-            c.wait_send()
+            c().wait_send()
+
+    def wait_recvs(copies):
+        for c in copies:
+            c().wait_recv()
 
     def sib_copy(j):
         return rcopy(ub.at[2 * j], sb.at[j], sib_s.at[j], sib_r.at[j], SIB)
@@ -106,7 +113,7 @@
         return rcopy(pb.at[j, rpos(p, h)], xb.at[6 * p + n], xs_s.at[6 * p + n], xs_r.at[6 * p + n], (UP, DN)[n % 2])
 
     def gpos(d, p, h):
-        return lanes(d * fc + p * fh + h * fq, fq)
+        return lanes(d * fc + p * 2 * fq + h * fq, fq)
 
     def y_rs(p, n):
         d, h = ((y_op, 0), (y_op, 1), (y_up, 1), (y_dn, 0), (y_up, 0), (y_dn, 1))[n]
@@ -119,29 +126,33 @@
             return rcopy(src, src, ss.at[6 * p + n], rs.at[6 * p + n], (up, dn)[n % 2])
         return copy
 
-    def xpos(d, p, h):
-        return (d * CORES + core) * rc + p * rh + h * rq
+    def cross(n):
+        src = rt.at[:, lanes(xpos((c_dn, c_up)[n], 1, n), rq)]
+        return rcopy(src, src, xp_s.at[8 + n], xp_r.at[8 + n], (UPX, DNX)[n])
+
+    def xpos(d, p, h, size=rq):
+        return (d * CORES + core) * rc + (2 * p + h) * size
 
     def wpos(d, p, h):
-        return srows(d * fc + p * fh + h * fq, fq)
+        return srows(d * fc + p * fh + h * fh // 2, fh // 2)
 
     y_ag = ring(lambda d, p, h: st.at[:, gpos(d, p, h)], yg_s, yg_r, YUP, YDN, yi, y_dn, y_up)
     x_ag = ring(lambda d, p, h: rt.at[:, lanes(xpos(d, p, h), rq)], xg_s, xg_r, UP, DN, chip, c_dn, c_up)
     w_ag = ring(lambda d, p, h: w_out.at[wpos(d, p, h), :], wg_s, wg_r, YUP, YDN, yi, y_dn, y_up)
-    r_ag = ring(lambda d, p, h: r_out.at[srows(xpos(d, p, h), rq), :], rg_s, rg_r, UP, DN, chip, c_dn, c_up)
-
-    def pair(at, ss, rs):
+    r_ag = ring(lambda d, p, h: r_out.at[erows(xpos(d, p, h, re), re), :], rg_s, rg_r, UP, DN, chip, c_dn, c_up)
+
+    def pair(at, unit, ss, rs):
         def copy(p, n):
-            d, h, size = ((chip, 0, rh), (c_dn, 0, rh), (c_up, 0, rh), (c_op, 0, rq), (c_op, 1, rq))[n]
-            src = at(xpos(d, p, h), size)
+            d, h, units = ((chip, 0, 2), (c_dn, 0, 2), (c_up, 0, 2), (c_op, 0, 1), (c_op, 1, 1))[n]
+            src = at(xpos(d, p, h, unit), units * unit)
             return rcopy(src, src, ss.at[5 * p + n], rs.at[5 * p + n], SIB)
         return copy
 
-    x_pair = pair(lambda o, n: rt.at[:, lanes(o, n)], xp_s, xp_r)
-    r_pair = pair(lambda o, n: r_out.at[srows(o, n), :], rp_s, rp_r)
-
-    def all_of(copy, n):
-        return [copy(p, i) for p in PIECES for i in range(n)]
+    x_pair = pair(lambda o, n: rt.at[:, lanes(o, n)], rq, xp_s, xp_r)
+    r_pair = pair(lambda o, n: r_out.at[erows(o, n), :], re, rp_s, rp_r)
+
+    def all_of(copy, n, pieces=PIECES):
+        return [functools.partial(copy, p, i) for p in pieces for i in range(n)]
 
     def start_own(ag, p):
         for n in range(4):
@@ -152,19 +163,37 @@
             ag(p, n).wait_recv()
             ag(p, n + 4).start()
 
-    def ring_and_pair(ag, pr):
-        for p in PIECES:
-            pass_on(ag, p)
+    def near(pr, p):
+        return [functools.partial(pr, p, n) for n in range(3)]
+
+    def far(pr, p):
+        return [functools.partial(pr, p, n) for n in (3, 4)]
+
+    crosses = [functools.partial(cross, 0), functools.partial(cross, 1)]
+
+    def ring_and_pair(ag, pr, pieces, crossed, meanwhile):
+        last = len(pieces) - 1
+        for p in pieces:
+            for n in range(2):
+                ag(p, n).wait_recv()
+                ag(p, n + 4).start()
+                if crossed and p == last:
+                    cross(n).start()
             ag(p, 2).wait_recv()
             pr(p, 1).start()
             ag(p, 3).wait_recv()
             pr(p, 2).start()
-        for p in PIECES:
+        for p in pieces:
+            if p == last:
+                wait_recvs([c for q in pieces for c in near(pr, q)])
+                if meanwhile is not None:
+                    meanwhile()
             for n in range(2):
                 ag(p, n + 4).wait_recv()
-                pr(p, n + 3).start()
-        for c in all_of(pr, 5):
-            c.wait_recv()
+                if not (crossed and p == last):
+                    pr(p, n + 3).start()
+        for p in pieces:
+            wait_recvs(crosses if crossed and p == last else far(pr, p))
 
     def combine():
         for p in PIECES:
@@ -204,16 +233,27 @@
         lax.fori_loop(0, nf, step, 0)
 
     def scatter_last():
-        for i in (0, 2, 4, 1, 6, 3, 5, 7):
-            j, who = i // 2, i % 2
-            u = last_product(i).astype(BF16)
-            if who == 0:
-                ub[i] = u
-                sib_copy(j).start()
-            else:
-                sib_copy(j).wait_recv()
-                pb[j] = u.astype(F32) + sb[j].astype(F32)
-                send_sums(j)
+        def make(i):
+            ub[i] = last_product(i).astype(BF16)
+            if i % 2 == 0:
+                sib_copy(i // 2).start()
+
+        def close(j):
+            sib_copy(j).wait_recv()
+            pb[j] = ub[2 * j + 1].astype(F32) + sb[j].astype(F32)
+            send_sums(j)
+
+        for i in (0, 1, 2):
+            make(i)
+        close(0)
+        make(4)
+        make(3)
+        close(1)
+        make(5)
+        close(2)
+        make(6)
+        make(7)
+        close(3)
         combine()
 
     def finish_piece(p, scale):
@@ -255,23 +295,38 @@
             rt[:, lanes(fi * rc + p * rh, rh)] = jnp.transpose(res[pl.ds(p * rh, rh)]).astype(BF16)
             start_own(x_ag, p)
             x_pair(p, 0).start()
-        wait_sends([sib_copy(j) for j in range(nx)])
+        wait_sends([functools.partial(sib_copy, j) for j in range(nx)])
         wait_sends(all_of(x_rs, 6))
-        ring_and_pair(x_ag, x_pair)
+        rows_of = CORES * rc
+
+        def chip_dot(d, col):
+            return jnp.dot(rt[:, lanes(d * rows_of, rows_of)], x[srows(d * rows_of, rows_of), col],
+                           preferred_element_type=F32)
+
+        def g_early():
+            for q in PIECES:
+                col = lanes(y_op * fc + q * fh, fh)
+                gp[:, col] = chip_dot(chip, col) + chip_dot(c_up, col) + chip_dot(c_dn, col)
+        ring_and_pair(x_ag, x_pair, PIECES, True, g_early)
+
+        for p in PIECES:
+            col = lanes(y_op * fc + p * fh, fh)
+            gp[:, col] = gp[:, col] + chip_dot(c_op, col)
+            y_rs(p, 0).start()
+            y_rs(p, 1).start()
 
         def g_step(i, c):
             j, q = i // 2, i % 2
             col = lanes(((yi + ring_off(j)) % ny) * fc + q * fh, fh)
             gp[:, col] = jnp.dot(rt[...], x[:, col], preferred_element_type=F32)
             for p in PIECES:
-                for jj, ns in ((0, (0, 1)), (1, (2,)), (2, (3,))):
+                for jj in (1, 2):
                     @pl.when(i == 2 * jj + p)
                     def _():
-                        for n in ns:
-                            y_rs(p, n).start()
+                        y_rs(p, jj + 1).start()
             return c
-        lax.fori_loop(0, 2 * ny, g_step, 0)
-        wait_sends(all_of(x_ag, 6) + all_of(x_pair, 5))
+        lax.fori_loop(2, 2 * ny, g_step, 0)
+        wait_sends(all_of(x_ag, 6) + near(x_pair, 0) + near(x_pair, 1) + far(x_pair, 0) + crosses)
         for p in PIECES:
             for n, d in ((0, y_up), (1, y_dn)):
                 y_rs(p, n).wait_recv()
@@ -284,7 +339,7 @@
                 y_rs(p, a).wait_recv()
                 y_rs(p, b).wait_recv()
                 own = gpos(yi, p, h)
-                wsl = pl.ds(p * fh + h * fq, fq)
+                wsl = pl.ds((2 * p + h) * fq, fq)
                 g = (gp[:, own] + yb[6 * p + a] + yb[6 * p + b]) * inv_total
                 w = wt[:, wsl]
                 s = eta_ref[:, own] * (g - lam_col[...] * w)
@@ -292,47 +347,53 @@
                 st[:, own] = s.astype(BF16)
             start_own(y_ag, p)
             part(yi, p, p == 0)
+
+        def own_in(p):
+            for n in (2, 3):
+                y_ag(p, n).wait_recv()
+
         pass_on(y_ag, 0)
-        for n in (2, 3):
-            y_ag(0, n).wait_recv()
+        own_in(0)
         part(y_dn, 0, False)
         pass_on(y_ag, 1)
+
+        @pl.when(k == SWEEPS - 1)
+        def _():
+            w_out[srows(yi * fc, fc), :] = jnp.transpose(wt[...])
+            for p in PIECES:
+                start_own(w_ag, p)
         part(y_up, 0, False)
-        for n in (2, 3):
-            y_ag(1, n).wait_recv()
+        own_in(1)
         part(y_dn, 1, False)
         part(y_up, 1, False)
         wait_sends(all_of(y_rs, 6))
 
-        @pl.when(k == SWEEPS - 1)
-        def _():
-            w_out[srows(yi * fc, fc), :] = jnp.transpose(wt[...])
         for p in PIECES:
             for n in (4, 5):
                 y_ag(p, n).wait_recv()
 
-        @pl.when(k == SWEEPS - 1)
-        def _():
-            for p in PIECES:
-                start_own(w_ag, p)
         scatter_last()
         wait_sends(all_of(y_ag, 6))
         return carry
 
     scatter_first()
+    lam_col[...] = jnp.transpose(jnp.broadcast_to(lam_ref[...], (lam_col.shape[1], targets)))
+    for h in range(2):
+        wt[:, pl.ds(h * fh, fh)] = jnp.transpose(w_out[srows(yi * fc + h * fh, fh), :])
+    y_copy.wait()
     lax.fori_loop(0, SWEEPS, sweep, 0)
 
+    for p in PIECES:
+        pass_on(w_ag, p)
     for p in PIECES:
         finish_piece(p, STEP_WEIGHT)
         r_out[srows(fi * rc + p * rh, rh), :] = res[pl.ds(p * rh, rh)]
         start_own(r_ag, p)
         r_pair(p, 0).start()
-    for p in PIECES:
-        pass_on(w_ag, p)
-    wait_sends([sib_copy(j) for j in range(nx)])
+    wait_sends([functools.partial(sib_copy, j) for j in range(nx)])
     wait_sends(all_of(x_rs, 6))
 
-    ring_and_pair(r_ag, r_pair)
+    ring_and_pair(r_ag, r_pair, PIECES, False, None)
     for p in PIECES:
         for n in range(2, 6):
             w_ag(p, n).wait_recv()
@@ -376,7 +437,7 @@
                 pltpu.VMEM((feats, nt), BF16),
                 pltpu.VMEM((nt, fc // 4), F32),
                 dma(nf), dma(2), dma(nx), dma(nx), dma(12), dma(12), dma(12), dma(12),
-                dma(12), dma(12), dma(10), dma(10), dma(12), dma(12), dma(12), dma(12), dma(12), dma(12), dma(10), dma(10),
+                dma(12), dma(12), dma(10), dma(10), dma(12), dma(12), dma(12), dma(12), dma(24), dma(24), dma(20), dma(20),
             ],
             compiler_params=pltpu.CompilerParams(
                 collective_id=0, has_side_effects=True, vmem_limit_bytes=54 * 1024 * 1024),

time: 240 us -> 237 us (0.988)
  Pallas kernels: 237 us -> 234 us
    pallas_call x1, Pallas kernels: 237 us -> 234 us  [local_sweeps(): pl.pallas_call(functools.partial(sweeps_kernel, ny, nf), out_shape=(pltpu...]
where the time goes in v3:
time: 237 us
  Pallas kernels  234 us (99%)
  local copies, waits for them, and re-layouts  2.64 us (1%)
    pallas_call x1, Pallas kernels, local_sweeps(): pl.pallas_call(functools.partial(sweeps_kernel, ny, nf), out_shape=(pltpu...  234 us

profile of v3, /device:TPU:97, one launch (start us, length us, event | category | flops | bytes accessed | tf_op | source)
XLA Modules:
  0.0 237.0 jit_solution(18191499864333398848)
XLA Ops:
  0.6 233.7 %sweeps.1 = (f32[4096,128]{1,0:T(8,128)S(1)}, f32[4096,128]{1,0:T(8,128)S(1)}) custom-call(bf16[4096,4096]{1,0:T(8,128)(2,1)} %x_hbm.1, f32[4096,128]{1,0:T(8,128)} %y_hbm.1, f32[4096,128]{1,0:T(8,128)} %w0_hbm.1, f32[1,4096]{1,0:T(1,128)} %bitcast.2, f32[1,128]{1,0:T(1,128)} %bitcast.3), custom_call_target="tpu_custom_call" | custom-call | tf_op jit(solution)/shard_map/sweeps/pallas_call | solution.py:419
  234.4 1.3 copy.9
  235.7 1.3 copy.10

commit v4 on v2

--- a/solution.py
+++ b/solution.py
@@ -40,6 +40,8 @@
     UP = {"feat": c_up * CORES + core}
     DN = {"feat": c_dn * CORES + core}
     SIB = {"feat": chip * CORES + 1 - core}
+    UPX = {"feat": c_up * CORES + 1 - core}
+    DNX = {"feat": c_dn * CORES + 1 - core}
     YUP = {"samp": y_up}
     YDN = {"samp": y_dn}
 
@@ -73,7 +75,7 @@
     y_copy.start()
 
     barrier = pltpu.get_barrier_semaphore()
-    peers = (UP, DN, SIB, YUP, YDN)
+    peers = (UP, DN, UPX, DNX, SIB, YUP, YDN)
     for dev in peers:
         pl.semaphore_signal(barrier, inc=1, device_id=dev, device_id_type=MESH)
 
@@ -119,6 +121,10 @@
             return rcopy(src, src, ss.at[6 * p + n], rs.at[6 * p + n], (up, dn)[n % 2])
         return copy
 
+    def cross(n):
+        src = rt.at[:, lanes(xpos((c_dn, c_up)[n], 1, n), rq)]
+        return rcopy(src, src, xp_s.at[8 + n], xp_r.at[8 + n], (UPX, DNX)[n])
+
     def xpos(d, p, h):
         return (d * CORES + core) * rc + p * rh + h * rq
 
@@ -143,6 +149,10 @@
     def all_of(copy, n):
         return [copy(p, i) for p in PIECES for i in range(n)]
 
+    def pairs(pr, crossed):
+        return [pr(0, n) for n in range(5)] + [pr(1, n) for n in range(3)] + (
+            [cross(0), cross(1)] if crossed else [pr(1, 3), pr(1, 4)])
+
     def start_own(ag, p):
         for n in range(4):
             ag(p, n).start()
@@ -152,18 +162,28 @@
             ag(p, n).wait_recv()
             ag(p, n + 4).start()
 
-    def ring_and_pair(ag, pr):
-        for p in PIECES:
-            pass_on(ag, p)
+    def ring_and_pair(ag, pr, crossed, meanwhile):
+        for p in PIECES:
+            for n in range(2):
+                ag(p, n).wait_recv()
+                ag(p, n + 4).start()
+                if crossed and p == 1:
+                    cross(n).start()
             ag(p, 2).wait_recv()
             pr(p, 1).start()
             ag(p, 3).wait_recv()
             pr(p, 2).start()
         for p in PIECES:
+            if p == 1:
+                for c in pairs(pr, crossed)[:3] + pairs(pr, crossed)[5:8]:
+                    c.wait_recv()
+                if meanwhile is not None:
+                    meanwhile()
             for n in range(2):
                 ag(p, n + 4).wait_recv()
-                pr(p, n + 3).start()
-        for c in all_of(pr, 5):
+                if not (crossed and p == 1):
+                    pr(p, n + 3).start()
+        for c in pairs(pr, crossed)[3:5] + pairs(pr, crossed)[8:]:
             c.wait_recv()
 
     def combine():
@@ -204,16 +224,27 @@
         lax.fori_loop(0, nf, step, 0)
 
     def scatter_last():
-        for i in (0, 2, 4, 1, 6, 3, 5, 7):
-            j, who = i // 2, i % 2
-            u = last_product(i).astype(BF16)
-            if who == 0:
-                ub[i] = u
-                sib_copy(j).start()
-            else:
-                sib_copy(j).wait_recv()
-                pb[j] = u.astype(F32) + sb[j].astype(F32)
-                send_sums(j)
+        def make(i):
+            ub[i] = last_product(i).astype(BF16)
+            if i % 2 == 0:
+                sib_copy(i // 2).start()
+
+        def close(j):
+            sib_copy(j).wait_recv()
+            pb[j] = ub[2 * j + 1].astype(F32) + sb[j].astype(F32)
+            send_sums(j)
+
+        for i in (0, 1, 2):
+            make(i)
+        close(0)
+        make(4)
+        make(3)
+        close(1)
+        make(5)
+        close(2)
+        make(6)
+        make(7)
+        close(3)
         combine()
 
     def finish_piece(p, scale):
@@ -257,21 +288,36 @@
             x_pair(p, 0).start()
         wait_sends([sib_copy(j) for j in range(nx)])
         wait_sends(all_of(x_rs, 6))
-        ring_and_pair(x_ag, x_pair)
+        rows_of = CORES * rc
+
+        def chip_dot(d, col):
+            return jnp.dot(rt[:, lanes(d * rows_of, rows_of)], x[srows(d * rows_of, rows_of), col],
+                           preferred_element_type=F32)
+
+        def g_early():
+            for q in PIECES:
+                col = lanes(y_op * fc + q * fh, fh)
+                gp[:, col] = chip_dot(chip, col) + chip_dot(c_up, col) + chip_dot(c_dn, col)
+        ring_and_pair(x_ag, x_pair, True, g_early)
+
+        for p in PIECES:
+            col = lanes(y_op * fc + p * fh, fh)
+            gp[:, col] = gp[:, col] + chip_dot(c_op, col)
+            y_rs(p, 0).start()
+            y_rs(p, 1).start()
 
         def g_step(i, c):
             j, q = i // 2, i % 2
             col = lanes(((yi + ring_off(j)) % ny) * fc + q * fh, fh)
             gp[:, col] = jnp.dot(rt[...], x[:, col], preferred_element_type=F32)
             for p in PIECES:
-                for jj, ns in ((0, (0, 1)), (1, (2,)), (2, (3,))):
+                for jj in (1, 2):
                     @pl.when(i == 2 * jj + p)
                     def _():
-                        for n in ns:
-                            y_rs(p, n).start()
+                        y_rs(p, jj + 1).start()
             return c
-        lax.fori_loop(0, 2 * ny, g_step, 0)
-        wait_sends(all_of(x_ag, 6) + all_of(x_pair, 5))
+        lax.fori_loop(2, 2 * ny, g_step, 0)
+        wait_sends(all_of(x_ag, 6) + pairs(x_pair, True))
         for p in PIECES:
             for n, d in ((0, y_up), (1, y_dn)):
                 y_rs(p, n).wait_recv()
@@ -332,7 +378,7 @@
     wait_sends([sib_copy(j) for j in range(nx)])
     wait_sends(all_of(x_rs, 6))
 
-    ring_and_pair(r_ag, r_pair)
+    ring_and_pair(r_ag, r_pair, False, None)
     for p in PIECES:
         for n in range(2, 6):
             w_ag(p, n).wait_recv()

time: 240 us -> 237 us (0.988)
  Pallas kernels: 237 us -> 233 us
    pallas_call x1, Pallas kernels: 237 us -> 233 us  [local_sweeps(): pl.pallas_call(functools.partial(sweeps_kernel, ny, nf), out_shape=(pltpu...]
where the time goes in v4:
time: 237 us
  Pallas kernels  233 us (98%)
  local copies, waits for them, and re-layouts  2.64 us (1%)
    pallas_call x1, Pallas kernels, local_sweeps(): pl.pallas_call(functools.partial(sweeps_kernel, ny, nf), out_shape=(pltpu...  233 us

profile of v4, /device:TPU:97, one launch (start us, length us, event | category | flops | bytes accessed | tf_op | source)
XLA Modules:
  0.0 236.7 jit_solution(5251408299700175227)
XLA Ops:
  0.6 233.4 %sweeps.1 = (f32[4096,128]{1,0:T(8,128)S(1)}, f32[4096,128]{1,0:T(8,128)S(1)}) custom-call(bf16[4096,4096]{1,0:T(8,128)(2,1)} %x_hbm.1, f32[4096,128]{1,0:T(8,128)} %y_hbm.1, f32[4096,128]{1,0:T(8,128)} %w0_hbm.1, f32[1,4096]{1,0:T(1,128)} %bitcast.2, f32[1,128]{1,0:T(1,128)} %bitcast.3), custom_call_target="tpu_custom_call" | custom-call | tf_op jit(solution)/shard_map/sweeps/pallas_call | solution.py:404
  234.0 1.3 copy.9
  235.3 1.3 copy.10
